TPU v7x, 128 devices: a whole 4x4x4 slice. The times are simulated.
128 devices in a mesh: gx: 8 (over x, core), gy: 16 (over z, y).
Axes of the slice: x: 4, y: 4, z: 4, core: 2. Of those that a mesh axis runs over, the one named last changes fastest.
Arguments:
- mask_feats: bfloat16 [256, 8, 14, 14, 256], P(('gx', 'gy')), may hold values from -6 to 6
- mask_cot: bfloat16 [256, 8, 14, 14, 256], P(('gx', 'gy')), may hold values from -6 to 6
- roi_counts: int32 [256], P(('gx', 'gy')), may hold values from 1 to 8, as said below
- rpn_feats: bfloat16 [256, 48, 32, 256], P(('gx', 'gy')), may hold values from -6 to 6
- rpn_cot: bfloat16 [256, 48, 32, 256], P(('gx', 'gy')), may hold values from -360 to 360
- anchor_counts: int32 [256], P(('gx', 'gy')), may hold values from 32 to 223
- mask_weight: float32 [2304, 256], replicated, may hold values from -0.125 to 0.125
- rpn_weight: float32 [2304, 256], replicated, may hold values from -0.125 to 0.125
- mask_moment: float32 [2304, 256], replicated, may hold values from -6 to 6
- rpn_moment: float32 [2304, 256], replicated, may hold values from -6 to 6
Outputs:
- new_mask_weight: float32 [2304, 256], replicated
- new_rpn_weight: float32 [2304, 256], replicated
- new_mask_moment: float32 [2304, 256], replicated
- new_rpn_moment: float32 [2304, 256], replicated
Inputs may be any that keep to these rules, and one draw needn't show every extreme that they name: `roi_counts`: every image has at least one positive ROI; some image has all 8 slots positive.
All inputs are finite; a program needn't handle non-finite values.
Results may differ from a plain program's by a relative error of at most 0.0003.
Values sent between devices are 32-bit elements; how exact they have to be, the bound alone decides.
No kernel may reach another device: no remote copies, remote signals or barrier semaphores. Data moves between devices by JAX's collectives and lax.ppermute only.
A program may use at most 128 MiB of HBM per device.

v0:
```python
import jax
import jax.numpy as jnp
from jax import lax
from jax.sharding import PartitionSpec as P


def weight_grad(feats, cotan):
    grid_rows = feats.shape[1]
    grid_cols = feats.shape[2]
    chans = feats.shape[3]
    padded = jnp.pad(feats, ((0, 0), (1, 1), (1, 1), (0, 0)))
    flat_cot = cotan.reshape(-1, chans)
    blocks = []
    for row_tap in range(3):
        for col_tap in range(3):
            window = padded[
                :, row_tap : row_tap + grid_rows, col_tap : col_tap + grid_cols, :
            ].reshape(-1, chans)
            blocks.append(
                lax.dot_general(
                    window, flat_cot, (((0,), (0,)), ((), ())), preferred_element_type=jnp.float32
                )
            )
    return jnp.concatenate(blocks, axis=0)


def step_update(weight, moment, grad):
    fresh_moment = 0.9 * moment + grad
    return (weight - 0.02 * fresh_moment, fresh_moment)


def on_device(
    mask_feats,
    mask_cot,
    roi_counts,
    rpn_feats,
    rpn_cot,
    anchor_counts,
    mask_weight,
    rpn_weight,
    mask_moment,
    rpn_moment,
):
    slot_count = mask_feats.shape[1]
    side = mask_feats.shape[2]
    chans = mask_feats.shape[4]
    slots = jnp.arange(slot_count, dtype=jnp.int32)
    valid_slots = (slots[None, :] < roi_counts[:, None]).astype(jnp.bfloat16)
    masked = mask_cot * valid_slots[:, :, None, None, None]
    mask_local = weight_grad(
        mask_feats.reshape(-1, side, side, chans), masked.reshape(-1, side, side, chans)
    )
    rpn_local = weight_grad(rpn_feats, rpn_cot)
    local_counts = jnp.stack([jnp.sum(roi_counts), jnp.sum(anchor_counts)]).astype(jnp.float32)
    mask_sum, rpn_sum, totals = lax.psum((mask_local, rpn_local, local_counts), ("gx", "gy"))
    mask_grad = mask_sum / totals[0]
    rpn_grad = rpn_sum / totals[1]
    new_mask_weight, new_mask_moment = step_update(mask_weight, mask_moment, mask_grad)
    new_rpn_weight, new_rpn_moment = step_update(rpn_weight, rpn_moment, rpn_grad)
    return (new_mask_weight, new_rpn_weight, new_mask_moment, new_rpn_moment)


def solution(mesh):
    placed = (
        P(("gx", "gy"), None, None, None, None),
        P(("gx", "gy"), None, None, None, None),
        P(("gx", "gy")),
        P(("gx", "gy"), None, None, None),
        P(("gx", "gy"), None, None, None),
        P(("gx", "gy")),
        P(),
        P(),
        P(),
        P(),
    )
    return jax.shard_map(
        on_device, mesh=mesh, in_specs=placed, out_specs=(P(), P(), P(), P()), check_vma=False
    )
```

profile of v0, /device:TPU:1, one launch (start us, length us, event | category | flops | bytes accessed | tf_op | source)
XLA Modules:
  0.0 269.6 jit_solution(1782575717403272848)
XLA Ops:
  11.3 3.7 %reshape_reshape.3 = bf16[3136,256]{1,0:T(8,128)(2,1)} reshape(bf16[2,8,14,14,256]{4,3,2,1,0:T(8,128)(2,1)} %copy.29) | data formatting | bytes 3211264 | tf_op jit(solution)/shard_map/reshape;reshape | solution.py:12
  16.5 4.3 %pad_slice_fusion = (bf16[16,14,14,256]{3,0,2,1:T(8,128)(2,1)}, bf16[16,14,14,256]{3,0,2,1:T(8,128)(2,1)}, bf16[16,14,14,256]{3,0,2,1:T(8,128)(2,1)}, bf16[16,14...) fusion(bf16[16,14,14,256]{3,0,2,1:T(8,128)(2,1)S(1)} %bitcast.89), kind=kLoop, calls=%fused_computation.4 | loop fusion | bytes 14450688 | tf_op jit(solution)/shard_map/slice | solution.py:16
  20.8 1.8 copy.28
  22.7 3.6 %reshape.70 = bf16[3136,256]{1,0:T(8,128)(2,1)} reshape(bf16[16,14,14,256]{3,2,1,0:T(8,128)(2,1)} %copy.28) | data formatting | bytes 3211264 | tf_op jit(solution)/shard_map/reshape | solution.py:18
  26.3 3.3 %copy.30 = bf16[16,14,14,256]{3,2,1,0:T(8,128)(2,1)} copy(bf16[16,14,14,256]{3,0,2,1:T(8,128)(2,1)} %get-tuple-element.11) | data formatting | bytes 3211264 | tf_op jit(solution)/shard_map/slice | solution.py:16
  29.6 3.6 %reshape.71 = bf16[3136,256]{1,0:T(8,128)(2,1)} reshape(bf16[16,14,14,256]{3,2,1,0:T(8,128)(2,1)} %copy.30) | data formatting | bytes 3211264 | tf_op jit(solution)/shard_map/reshape | solution.py:18
  33.2 3.3 %copy.31 = bf16[16,14,14,256]{3,2,1,0:T(8,128)(2,1)} copy(bf16[16,14,14,256]{3,0,2,1:T(8,128)(2,1)} %get-tuple-element.12) | data formatting | bytes 3211264 | tf_op jit(solution)/shard_map/slice | solution.py:16
  36.5 3.6 %reshape.72 = bf16[3136,256]{1,0:T(8,128)(2,1)} reshape(bf16[16,14,14,256]{3,2,1,0:T(8,128)(2,1)} %copy.31) | data formatting | bytes 3211264 | tf_op jit(solution)/shard_map/reshape | solution.py:18
  40.1 3.3 %copy.32 = bf16[16,14,14,256]{3,2,1,0:T(8,128)(2,1)} copy(bf16[16,14,14,256]{3,0,2,1:T(8,128)(2,1)} %get-tuple-element.13) | data formatting | bytes 3211264 | tf_op jit(solution)/shard_map/slice | solution.py:16
  43.3 3.6 %reshape.73 = bf16[3136,256]{1,0:T(8,128)(2,1)} reshape(bf16[16,14,14,256]{3,2,1,0:T(8,128)(2,1)} %copy.32) | data formatting | bytes 3211264 | tf_op jit(solution)/shard_map/reshape | solution.py:18
  47.0 3.4 %convolution_dynamic-update-slice_fusion.7 = f32[2304,256]{1,0:T(8,128)} fusion(bf16[3136,256]{1,0:T(8,128)(2,1)} %reshape.70, bf16[3136,256]{1,0:T(8,128)(2,1)} %reshape_reshape.3), kind=kOutput, calls=%fused_computation.36 | convolution fusion | flops 411041792 | bytes 3473408 | tf_op jit(solution)/shard_map/dot_general | solution.py:20
  58.2 2.0 copy.36
  61.6 2.0 copy.37
  65.0 2.0 copy.38
  68.5 2.3 copy.39
  70.8 1.8 fusion.24
  72.6 2.1 fusion.22
  74.7 2.0 fusion.20
  80.1 2.1 fusion.14
  82.2 2.3 fusion.12
  84.5 2.1 fusion.10
  96.5 69.6 %psum.22 = f32[2]{0:T(128)S(1)} all-reduce(f32[2]{0:T(128)S(1)} %add_convert_fusion), channel_id=1, replica_groups=mesh['gx'=8,'gy'=16] {'gx','gy'}, use_global_device_ids=true, to_apply=%region_3.4 | all-reduce | flops 2 | bytes 16 | tf_op jit(solution)/shard_map/psum | solution.py:55
  166.7 85.5 %all-reduce.5.cloned.1.call-done = (f32[2304,256]{1,0:T(8,128)}, f32[2304,256]{1,0:T(8,128)}) async-done(((f32[2304,256]{1,0:T(8,128)}, f32[2304,256]{1,0:T(8,128)}), (f32[2304,256]{1,0:T(8,128)}, f32[2304,256]{1,0:T(8,128)})) %all-reduce.5.cloned.1.call-update) | async-done | bytes 4718608 | tf_op jit(solution)/shard_map/psum | solution.py:55
  252.2 10.6 %multiply_subtract_fusion = (f32[2304,256]{1,0:T(8,128)}, f32[2304,256]{1,0:T(8,128)}, f32[2304,256]{1,0:T(8,128)}, f32[2304,256]{1,0:T(8,128)}) fusion(f32[2304,256]{1,0:T(8,128)} %param.17, f32[2304,256]{1,0:T(8,128)} %get-tuple-element.5, f32[]{:T(128)} %bitcast.25, f32[2304,256]{1,0:T(8,128)} %param.19, f32[2304,256]{1,0:T(8,128)} %param.16, ...), kind=kLoop, calls=%fused_computation | loop fusion | flops 5898240 | bytes 23592968 | tf_op jit(solution)/shard_map/sub | solution.py:29
  (58 shorter events, 31.5 us)
Async XLA Ops:
  7.2 63.6 %copy-start = (bf16[2,48,32,256]{3,2,1,0:T(8,128)(2,1)S(1)}, bf16[2,48,32,256]{3,2,1,0:T(8,128)(2,1)}, u32[]{:S(2)}) copy-start(bf16[2,48,32,256]{3,2,1,0:T(8,128)(2,1)} %param.14) | copy-start | bytes 4718596
  7.2 245.1 %all-reduce.5.cloned.1.call-start = ((), (), s32[]{:S(2)}) async-start(), calls=%async_computation | async-start | bytes 9437184 | tf_op jit(solution)/shard_map/psum | solution.py:55
  47.0 3.4 %copy-start.5 = (bf16[3136,256]{1,0:T(8,128)(2,1)S(1)}, bf16[3136,256]{1,0:T(8,128)(2,1)}, u32[]{:S(2)}) copy-start(bf16[3136,256]{1,0:T(8,128)(2,1)} %reshape_reshape.3) | copy-start | bytes 4816900
  47.0 3.4 %copy-start.11 = (bf16[3136,256]{1,0:T(8,128)(2,1)S(1)}, bf16[3136,256]{1,0:T(8,128)(2,1)}, u32[]{:S(2)}) copy-start(bf16[3136,256]{1,0:T(8,128)(2,1)} %reshape.71) | copy-start | bytes 4816900
  50.4 1.4 copy-start.12
  51.8 1.4 copy-start.13
  53.2 1.4 copy-start.2
  54.6 1.5 copy-start.1
  76.7 1.4 copy-start.3
  84.5 2.1 copy-start.6
  84.5 2.1 copy-start.7
  86.6 1.5 copy-start.4
  86.6 2.4 copy-start.8
  89.0 1.4 copy-start.9
  90.4 1.4 copy-start.10
  93.2 0.7 copy-start.14
  93.2 1.3 copy-start.15
Sparse Core Ops, SparseCore 0:
  93.3 158.8 all-reduce.4
where the time goes:
time: 271 us; the launch traced here: 270 us
  waiting for transfers between devices  85.5 us (32%)
  blocking collectives  69.6 us (26%)
  local copies, waits for them, and re-layouts  54.6 us (20%)
  matrix products  30 us (11%)
  other arithmetic  15.6 us (6%)
  between operations  14.2 us (5%)
    psum x1, waiting for transfers between devices, on_device(): lax.psum((mask_local, rpn_local, local_counts), ('gx', 'gy'))  85.5 us
    psum x1, blocking collectives, on_device(): lax.psum((mask_local, rpn_local, local_counts), ('gx', 'gy'))  69.6 us
    dot_general x18, matrix products, weight_grad(): lax.dot_general(window, flat_cot, (((0,), (0,)), ((), ())), preferred_ele...  30 us
    slice x9, local copies, waits for them, and re-layouts, weight_grad(): padded[:, row_tap:row_tap + grid_rows, col_tap:col_tap + grid_cols, :]  22.6 us
    reshape x8, local copies, waits for them, and re-layouts, weight_grad(): window = padded[:, row_tap:row_tap + grid_rows, col_tap:col_tap + grid_co...  20.2 us
    sub x1, other arithmetic, step_update(): return (weight - 0.02 * fresh_moment, fresh_moment)  10.6 us
    unnamed x34, local copies, waits for them, and re-layouts  5.92 us
  transfers between devices with their start and end apart: 1, of which 1 were waited for; matrix products, arithmetic and copies ran while one was open for 1% of the time, Pallas kernels for 0%

commit v1 on v0

v1 whole, which is shorter than its diff:
```python
import functools

import jax
import jax.numpy as jnp
from jax import lax
from jax.experimental import pallas as pl
from jax.experimental.pallas import tpu as pltpu
from jax.sharding import PartitionSpec as P


AXES = ("gx", "gy")
DEVICES = 128
C = 256
SUB = 32
VM = pltpu.VMEM
HBM = pltpu.HBM

CHAINS = {
    "A": ("xyz", 0, (0, 3, 6, 1, 4, 7, 2), ()),
    "B": ("yzx", 1, (5, 8), (0, 3, 6, 1)),
    "C": ("zxy", 0, (), (4, 7, 2, 5, 8)),
}
SPLIT = 2


def coords(i):
    return {"x": i // 32, "core": (i // 16) % 2, "z": (i // 4) % 4, "y": i % 4}


def linear(d):
    return d["x"] * 32 + d["core"] * 16 + d["z"] * 4 + d["y"]


def partner(i, axis, step, lead):
    d = coords(i)
    half = (d["core"] + d["x"] + d["y"] + d["z"]) % 2
    if axis != "core":
        d[axis] ^= 1 if step == half ^ lead else 3
    d["core"] ^= 1
    return linear(d)


def swap(name, v, axis, step=0):
    pairs = [(i, partner(i, axis, step, CHAINS[name][1])) for i in range(DEVICES)]
    return lax.ppermute(v, AXES, pairs)


def block_id(name):
    order, lead = CHAINS[name][:2]
    gx, gy = lax.axis_index("gx"), lax.axis_index("gy")
    places = {"x": gx // 2, "z": gy // 4, "y": gy % 4}
    own = (gx + places["x"] + places["y"] + places["z"]) % 2
    at = places[order[0]]
    high = at // 2
    gray = (high + at) % 2
    one, two = gray * 2 + high, high * 2 + gray
    return (
        own * 4,
        (1 - own) * 4,
        jnp.where(own == lead, one, two),
        jnp.where(own == lead, two, one),
    )


def rows_of(where, q):
    base, partner_base, low, partner_low = where
    own = pl.multiple_of((base + (low ^ q)) * SUB, SUB)
    other = pl.multiple_of((partner_base + (partner_low ^ q)) * SUB, SUB)
    return pl.ds(own, SUB), pl.ds(other, SUB)


def put(buf, grad, where, keep, send, slot):
    buf[...] = grad
    for q in range(4):
        own, other = rows_of(where, q)
        keep[q, pl.ds(slot * SUB, SUB), :] = buf[own, :]
        send[q, pl.ds(slot * SUB, SUB), :] = buf[other, :]


def dot_t(a, b):
    return lax.dot_general(a, b, (((0,), (0,)), ((), ())), preferred_element_type=jnp.float32)


def columns_of(taps):
    return sorted({t % 3 for t in taps})


def load_mask(taps, roi, x, y, xp, yp):
    row = 14 * 8
    columns = columns_of(taps)
    zero = jnp.zeros((row, C), jnp.bfloat16)
    for k in range(len(columns)):
        for j in (0, 15, 30):
            xp[k, j * row : (j + 1) * row, :] = zero
    yp[14 * row : 15 * row, :] = zero
    slot = lax.broadcasted_iota(jnp.int32, (row, C), 0) % 8
    edge = jnp.zeros((8, C), jnp.bfloat16)
    for i in range(2):
        live = slot < roi[i]
        for r in range(14):
            v = x[i, r]
            shifted = (
                jnp.concatenate([edge, v[: row - 8]], 0),
                v,
                jnp.concatenate([v[8:], edge], 0),
            )
            at = (i * 15 + r + 1) * row
            for k, b in enumerate(columns):
                xp[k, at : at + row, :] = shifted[b]
            yp[at - row : at, :] = jnp.where(live, y[i, r], zero)


def mask_tap(t, taps, xp, yp):
    row, a, k = 14 * 8, t // 3, columns_of(taps).index(t % 3)
    return dot_t(xp[k, a * row : (a + 29) * row, :], yp[...])


def load_rpn(taps, x, xp):
    row = 32
    columns = columns_of(taps)
    zero = jnp.zeros((row, C), jnp.bfloat16)
    for k in range(len(columns)):
        for j in (0, 49, 98):
            xp[k, j * row : (j + 1) * row, :] = zero
    at_col = lax.broadcasted_iota(jnp.int32, (row, C), 0)
    for i in range(2):

        def shift(r, carry):
            v = x[i, r]
            at = pl.multiple_of((i * 49 + 1 + r) * row, row)
            wide = v.astype(jnp.float32)
            for k, b in enumerate(columns):
                if b == 1:
                    moved = v
                elif b == 0:
                    moved = jnp.where(at_col == 0, 0.0, pltpu.roll(wide, 1, 0))
                else:
                    moved = jnp.where(at_col == row - 1, 0.0, pltpu.roll(wide, row - 1, 0))
                xp[k, pl.ds(at, row), :] = moved.astype(jnp.bfloat16)
            return carry

        lax.fori_loop(0, 48, shift, 0, unroll=8)


def rpn_tap(t, taps, xp, y):
    row, a, k = 32, t // 3, columns_of(taps).index(t % 3)
    parts = [
        dot_t(
            xp[k, (i * 49 + a) * row : (i * 49 + a + 48) * row, :], y[i].reshape(48 * row, C)
        )
        for i in range(2)
    ]
    return parts[0] + parts[1]


def grads_mask_kernel(counts, x, y, keep_a, send_a, keep_b, send_b, xp, yp, buf):
    taps_a, taps_b = CHAINS["A"][2], CHAINS["B"][2]
    taps = taps_a + taps_b
    load_mask(taps, counts, x, y, xp, yp)
    where_a, where_b = block_id("A"), block_id("B")
    for k, t in enumerate(taps_a):
        put(buf, mask_tap(t, taps, xp, yp), where_a, keep_a, send_a, k)
    for k, t in enumerate(taps_b):
        put(buf, mask_tap(t, taps, xp, yp), where_b, keep_b, send_b, k)
    lane = lax.broadcasted_iota(jnp.int32, (8, C), 1)
    roi_sum = (counts[0] + counts[1]).astype(jnp.float32)
    anchor_sum = (counts[2] + counts[3]).astype(jnp.float32)
    sums = jnp.where(lane == 0, roi_sum, anchor_sum)
    for q in range(4):
        keep_a[q, len(taps_a) * SUB :, :] = sums
        send_a[q, len(taps_a) * SUB :, :] = sums


def grads_rpn_kernel(name, x, y, *refs):
    had, (keep, send, xp, buf) = refs[:-4], refs[-4:]
    rows = len(CHAINS[name][2]) * SUB
    if had:
        keep[:, :rows, :] = had[0][...]
        send[:, :rows, :] = had[1][...]
    taps = CHAINS[name][3]
    load_rpn(taps, x, xp)
    where = block_id(name)
    for k, t in enumerate(taps):
        put(buf, rpn_tap(t, taps, xp, y), where, keep, send, k + len(CHAINS[name][2]))


def whole():
    return pl.BlockSpec(memory_space=VM)


def f32(*shape):
    return jax.ShapeDtypeStruct(shape, jnp.float32)


def cost(mask, rpn):
    flops = 2 * C * C * (3136 * mask + 3072 * rpn)
    return pl.CostEstimate(flops=flops, bytes_accessed=4_000_000, transcendentals=0)


def grads_mask(roi, anchor, x, y):
    n_a, n_b = len(CHAINS["A"][2]), len(CHAINS["B"][2])
    shape_a, shape_b = f32(4, n_a * SUB + 8, C), f32(4, n_b * SUB, C)
    return pl.pallas_call(
        grads_mask_kernel,
        name="grads_a",
        out_shape=(shape_a, shape_a, shape_b, shape_b),
        in_specs=[pl.BlockSpec(memory_space=pltpu.SMEM)] + [whole()] * 2,
        out_specs=[whole()] * 4,
        scratch_shapes=[
            VM((3, 31 * 112, C), jnp.bfloat16),
            VM((29 * 112, C), jnp.bfloat16),
            VM((C, C), jnp.float32),
        ],
        compiler_params=pltpu.CompilerParams(vmem_limit_bytes=20 << 20),
        cost_estimate=cost(n_a + n_b, 0),
    )(jnp.concatenate([roi, anchor]), x, y)


def grads_rpn(name, x, y, had):
    rows = (len(CHAINS[name][2]) + len(CHAINS[name][3])) * SUB
    return pl.pallas_call(
        functools.partial(grads_rpn_kernel, name),
        out_shape=(f32(4, rows, C), f32(4, rows, C)),
        in_specs=[whole()] * (2 + len(had)),
        out_specs=[whole()] * 2,
        scratch_shapes=[
            VM((len(columns_of(CHAINS[name][3])), 99 * 32, C), jnp.bfloat16),
            VM((C, C), jnp.float32),
        ],
        compiler_params=pltpu.CompilerParams(vmem_limit_bytes=20 << 20),
        cost_estimate=cost(0, len(CHAINS[name][3])),
    )(x, y, *had)


def reduced(name, keep, send):
    keep = keep + swap(name, send, "core")
    steps = [(axis, s) for axis in CHAINS[name][0] for s in (0, 1)]
    for axis, s in steps[:SPLIT]:
        half = keep.shape[0] // 2
        keep = keep[:half] + swap(name, keep[half:], axis, s)
    for axis, s in steps[SPLIT:]:
        keep = keep + swap(name, keep, axis, s)
    for axis, s in reversed(steps[:SPLIT]):
        keep = jnp.concatenate([keep, swap(name, keep, axis, s)], 0)
    return keep, swap(name, keep, "core")


def update_kernel(name, taps, first, lane, own, other, counts, w, m, *refs):
    new_w, new_m, ow, om, buf, sem = refs[-6:]
    where = block_id(name)
    total = counts[0, 0:1, lane : lane + 1]
    copies = []
    for k, t in enumerate(taps):
        at = (first + k) * SUB
        for q in range(4):
            mine, theirs = rows_of(where, q)
            buf[mine, :] = own[q, at : at + SUB, :]
            buf[theirs, :] = other[q, at : at + SUB, :]
        rows = slice(t * C, (t + 1) * C)
        moment = 0.9 * m[rows, :] + buf[...] / total
        om[k] = moment
        ow[k] = w[rows, :] - 0.02 * moment
        copies.append(pltpu.make_async_copy(om.at[k], new_m.at[rows], sem.at[0, k]))
        copies.append(pltpu.make_async_copy(ow.at[k], new_w.at[rows], sem.at[1, k]))
        copies[-2].start()
        copies[-1].start()
    for c in copies:
        c.wait()


def update(name, taps, first, lane, own, other, counts, w, m, into):
    n = len(taps)
    return pl.pallas_call(
        functools.partial(update_kernel, name, taps, first, lane),
        out_shape=(f32(9 * C, C), f32(9 * C, C)),
        in_specs=[whole()] * 5 + [pl.BlockSpec(memory_space=HBM)] * len(into),
        out_specs=[pl.BlockSpec(memory_space=HBM)] * 2,
        scratch_shapes=[
            VM((n, C, C), jnp.float32),
            VM((n, C, C), jnp.float32),
            VM((C, C), jnp.float32),
            pltpu.SemaphoreType.DMA((2, n)),
        ],
        input_output_aliases={5: 0, 6: 1} if into else {},
        compiler_params=pltpu.CompilerParams(vmem_limit_bytes=8 << 20),
        cost_estimate=pl.CostEstimate(
            flops=1_000_000 * n, bytes_accessed=1_000_000 * n, transcendentals=0
        ),
    )(own, other, counts, w, m, *into)


def on_device(mf, mc, roi, rf, rc, anchor, mw, rw, mm, rm):
    x = jnp.transpose(mf, (0, 2, 3, 1, 4)).reshape(2, 14, 112, C)
    y = jnp.transpose(mc, (0, 2, 3, 1, 4)).reshape(2, 14, 112, C)
    *local_a, had_keep, had_send = grads_mask(roi, anchor, x, y)
    local_b = grads_rpn("B", rf, rc, (had_keep, had_send))
    local_c = grads_rpn("C", rf, rc, ())
    sums = {name: reduced(name, *local) for name, local in zip("ABC", (local_a, local_b, local_c))}
    counts = sums["A"][0][:1, len(CHAINS["A"][2]) * SUB :]
    new_mask, new_rpn = (), ()
    for name, (order, lead, mask_taps, rpn_taps) in CHAINS.items():
        own, other = sums[name]
        if mask_taps:
            new_mask = update(name, mask_taps, 0, 0, own, other, counts, mw, mm, new_mask)
        if rpn_taps:
            first = len(mask_taps)
            new_rpn = update(name, rpn_taps, first, 1, own, other, counts, rw, rm, new_rpn)
    return new_mask[0], new_rpn[0], new_mask[1], new_rpn[1]


def solution(mesh):
    split = P(AXES)
    placed = (split,) * 6 + (P(),) * 4
    return jax.shard_map(
        on_device, mesh=mesh, in_specs=placed, out_specs=(P(),) * 4, check_vma=False
    )
```

time: 271 us -> 98.1 us (0.36)
  blocking collectives: 69.6 us -> 0 us
  waiting for transfers between devices: 85.5 us -> 18.4 us
  starting transfers between devices: 0.04 us -> 55.3 us
  local copies, waits for them, and re-layouts: 54.6 us -> 4.58 us
  matrix products: 30 us -> 0 us
  Pallas kernels: 0 us -> 16.6 us
  other arithmetic: 15.6 us -> 1.94 us
  between operations: 14.2 us -> 1.07 us
    psum x1 -> x0, waiting for transfers between devices: 85.5 us -> none  [on_device(): lax.psum((mask_local, rpn_local, local_counts), ('gx', 'gy'))]
    psum x1 -> x0, blocking collectives: 69.6 us -> none  [on_device(): lax.psum((mask_local, rpn_local, local_counts), ('gx', 'gy'))]
    ppermute x0 -> x30, starting transfers between devices: none -> 55.3 us  [swap(): return lax.ppermute(v, AXES, pairs)]
    dot_general x18 -> x0, matrix products: 30 us -> none  [weight_grad(): lax.dot_general(window, flat_cot, (((0,), (0,)), ((), ())), preferred_ele...]
    slice x10 -> x7, local copies, waits for them, and re-layouts: 23.3 us -> 0.13 us  [the longest x6 0.13 us: reduced(): keep = keep[:half] + swap(name, keep[half:], axis, s)]
    reshape x8 -> x0, local copies, waits for them, and re-layouts: 20.2 us -> none  [weight_grad(): window = padded[:, row_tap:row_tap + grid_rows, col_tap:col_tap + grid_co...]
    ppermute x0 -> x30, waiting for transfers between devices: none -> 18.4 us  [swap(): return lax.ppermute(v, AXES, pairs)]
    pallas_call x0 -> x7, Pallas kernels: none -> 16.6 us  [the longest x4 6.46 us: update(): pl.pallas_call(functools.partial(update_kernel, name, taps, first, lane),...]
  transfers between devices with their start and end apart: 1 -> 30, of which waited for: 1 -> 12; matrix products, arithmetic and copies ran while one was open for 1% -> 1% of each run, Pallas kernels for 0% -> 9%
where the time goes in v1:
time: 98.1 us; the launch traced here: 98 us
  starting transfers between devices  55.3 us (56%)
  waiting for transfers between devices  18.4 us (19%)
  Pallas kernels  16.6 us (17%)
  local copies, waits for them, and re-layouts  4.58 us (5%)
  other arithmetic  1.94 us (2%)
  between operations  1.07 us (1%)
    ppermute x30, starting transfers between devices, swap(): return lax.ppermute(v, AXES, pairs)  55.3 us
    ppermute x30, waiting for transfers between devices, swap(): return lax.ppermute(v, AXES, pairs)  18.4 us
    pallas_call x4, Pallas kernels, update(): pl.pallas_call(functools.partial(update_kernel, name, taps, first, lane),...  6.46 us
    pallas_call x2, Pallas kernels, grads_rpn(): pl.pallas_call(functools.partial(grads_rpn_kernel, name), out_shape=(f32(...  5.24 us
    pallas_call x1, Pallas kernels, grads_mask(): pl.pallas_call(grads_mask_kernel, name='grads_a', out_shape=(shape_a, sha...  4.91 us
    unnamed x16, local copies, waits for them, and re-layouts  4.45 us
  transfers between devices with their start and end apart: 30, of which 12 were waited for; matrix products, arithmetic and copies ran while one was open for 1% of the time, Pallas kernels for 9%

profile of v1, /device:TPU:1, one launch (start us, length us, event | category | flops | bytes accessed | tf_op | source)
XLA Modules:
  0.0 98.0 jit_solution(16893658759735162127)
XLA Ops:
  4.2 4.9 %grads_a.1 = (f32[4,232,256]{2,1,0:T(8,128)S(1)}, f32[4,232,256]{2,1,0:T(8,128)S(1)}, f32[4,64,256]{2,1,0:T(8,128)S(1)}, f32[4,64,256]{2,1,0:T(8,128)S(1)}) custom-call(s32[4]{0:T(128)S(1)} %pad_add_fusion.counts, bf16[2,14,112,256]{3,2,1,0:T(8,128)(2,1)S(1)} %bitcast.6, bf16[2,14,112,256]{3,2,1,0:T(8,128)(2,1)S(1)} %bitcast.7), custom_call_target="tpu_custom_call" | custom-call | flops 3699376128 | bytes 4000000 | tf_op jit(solution)/shard_map/grads_a/pallas_call | solution.py:203
  10.6 2.4 %shard_map.129 = (f32[4,192,256]{2,1,0:T(8,128)S(1)}, f32[4,192,256]{2,1,0:T(8,128)S(1)}) custom-call(bf16[2,48,32,256]{3,2,1,0:T(8,128)(2,1)S(1)} %copy-done.6, bf16[2,48,32,256]{3,2,1,0:T(8,128)(2,1)S(1)} %copy-done.7, f32[4,64,256]{2,1,0:T(8,128)S(1)} %get-tuple-element.20.refs_0_, f32[4,64,256]{2,1,0:T(8,128)S(1)} %get-tuple-element.21.refs_1_), custom_call_target="tpu_custom_call" | custom-call | flops 1610612736 | bytes 4000000 | tf_op jit(solution)/shard_map/pallas_call | solution.py:221
  13.1 2.8 %shard_map.132 = (f32[4,160,256]{2,1,0:T(8,128)S(1)}, f32[4,160,256]{2,1,0:T(8,128)S(1)}) custom-call(bf16[2,48,32,256]{3,2,1,0:T(8,128)(2,1)S(1)} %copy-done.6, bf16[2,48,32,256]{3,2,1,0:T(8,128)(2,1)S(1)} %copy-done.7), custom_call_target="tpu_custom_call" | custom-call | flops 2013265920 | bytes 4000000 | tf_op jit(solution)/shard_map/pallas_call | solution.py:221
  16.7 2.6 %collective-permute-start.11 = (f32[2,232,256]{2,1,0:T(8,128)S(1)}, f32[2,232,256]{2,1,0:T(8,128)S(1)}, u32[]{:S(2)}, u32[]{:S(2)}) collective-permute-start(f32[2,232,256]{2,1,0:T(8,128)S(1)} %slice.57), channel_id=1, source_target_pairs={{0,48},{1,113},{2,50},{3,115},{4,116},{5,53},{6,118},{7,55},{8,56}... | collective-permute-start | bytes 1425416 | tf_op jit(solution)/shard_map/ppermute | solution.py:45
  21.3 3.8 %collective-permute-start.21 = (f32[2,160,256]{2,1,0:T(8,128)S(1)}, f32[2,160,256]{2,1,0:T(8,128)S(1)}, u32[]{:S(2)}, u32[]{:S(2)}) collective-permute-start(f32[2,160,256]{2,1,0:T(8,128)S(1)} %slice.62), channel_id=1, source_target_pairs={{0,20},{1,29},{2,22},{3,31},{4,24},{5,17},{6,26},{7,19},{8,28},{9,... | collective-permute-start | bytes 983048 | tf_op jit(solution)/shard_map/ppermute | solution.py:45
  27.1 2.9 %collective-permute-start.2 = (f32[1,192,256]{2,1,0:T(8,128)S(1)}, f32[1,192,256]{2,1,0:T(8,128)S(1)}, u32[]{:S(2)}, u32[]{:S(2)}) collective-permute-start(f32[1,192,256]{2,1,0:T(8,128)S(1)} %slice.55), channel_id=1, source_target_pairs={{0,17},{1,18},{2,19},{3,16},{4,23},{5,20},{6,21},{7,22},{8,25},{9,... | collective-permute-start | bytes 589832 | tf_op jit(solution)/shard_map/ppermute | solution.py:45
  30.0 2.4 %collective-permute-done.12 = f32[1,232,256]{2,1,0:T(8,128)S(1)} collective-permute-done((f32[1,232,256]{2,1,0:T(8,128)S(1)}, f32[1,232,256]{2,1,0:T(8,128)S(1)}, u32[]{:S(2)}, u32[]{:S(2)}) %collective-permute-start.12) | collective-permute-done | bytes 237600 | tf_op jit(solution)/shard_map/ppermute | solution.py:45
  32.4 2.2 %collective-permute-start.13 = (f32[1,232,256]{2,1,0:T(8,128)S(1)}, f32[1,232,256]{2,1,0:T(8,128)S(1)}, u32[]{:S(2)}, u32[]{:S(2)}) collective-permute-start(f32[1,232,256]{2,1,0:T(8,128)S(1)} %slice_add_fusion.3), channel_id=1, source_target_pairs={{0,17},{1,18},{2,19},{3,16},{4,23},{5,20},{6,21},{7,22},{8,25},{9,... | collective-permute-start | bytes 712712 | tf_op jit(solution)/shard_map/ppermute | solution.py:45
  34.7 2.9 %collective-permute-start.3 = (f32[1,192,256]{2,1,0:T(8,128)S(1)}, f32[1,192,256]{2,1,0:T(8,128)S(1)}, u32[]{:S(2)}, u32[]{:S(2)}) collective-permute-start(f32[1,192,256]{2,1,0:T(8,128)S(1)} %slice_add_fusion.4), channel_id=1, source_target_pairs={{0,28},{1,21},{2,30},{3,23},{4,16},{5,25},{6,18},{7,27},{8,20},{9,... | collective-permute-start | bytes 589832 | tf_op jit(solution)/shard_map/ppermute | solution.py:45
  37.5 2.0 %collective-permute-done.13 = f32[1,232,256]{2,1,0:T(8,128)S(1)} collective-permute-done((f32[1,232,256]{2,1,0:T(8,128)S(1)}, f32[1,232,256]{2,1,0:T(8,128)S(1)}, u32[]{:S(2)}, u32[]{:S(2)}) %collective-permute-start.13) | collective-permute-done | bytes 237600 | tf_op jit(solution)/shard_map/ppermute | solution.py:45
  39.7 1.9 %collective-permute-start.22 = (f32[1,160,256]{2,1,0:T(8,128)S(1)}, f32[1,160,256]{2,1,0:T(8,128)S(1)}, u32[]{:S(2)}, u32[]{:S(2)}) collective-permute-start(f32[1,160,256]{2,1,0:T(8,128)S(1)} %slice.64), channel_id=1, source_target_pairs={{0,28},{1,21},{2,30},{3,23},{4,16},{5,25},{6,18},{7,27},{8,20},{9,... | collective-permute-start | bytes 491528 | tf_op jit(solution)/shard_map/ppermute | solution.py:45
  41.6 3.2 %collective-permute-start.4 = (f32[1,192,256]{2,1,0:T(8,128)S(1)}, f32[1,192,256]{2,1,0:T(8,128)S(1)}, u32[]{:S(2)}, u32[]{:S(2)}) collective-permute-start(f32[1,192,256]{2,1,0:T(8,128)S(1)} %add.66), channel_id=1, source_target_pairs={{0,20},{1,29},{2,22},{3,31},{4,24},{5,17},{6,26},{7,19},{8,28},{9,... | collective-permute-start | bytes 589832 | tf_op jit(solution)/shard_map/ppermute | solution.py:45
  45.2 3.7 %collective-permute-start.15 = (f32[1,232,256]{2,1,0:T(8,128)S(1)}, f32[1,232,256]{2,1,0:T(8,128)S(1)}, u32[]{:S(2)}, u32[]{:S(2)}) collective-permute-start(f32[1,232,256]{2,1,0:T(8,128)S(1)} %add.74), channel_id=1, source_target_pairs={{0,20},{1,29},{2,22},{3,31},{4,24},{5,17},{6,26},{7,19},{8,28},{9,... | collective-permute-start | bytes 712712 | tf_op jit(solution)/shard_map/ppermute | solution.py:45
  49.0 2.8 %collective-permute-start.23 = (f32[1,160,256]{2,1,0:T(8,128)S(1)}, f32[1,160,256]{2,1,0:T(8,128)S(1)}, u32[]{:S(2)}, u32[]{:S(2)}) collective-permute-start(f32[1,160,256]{2,1,0:T(8,128)S(1)} %slice_add_fusion.5), channel_id=1, source_target_pairs={{0,48},{1,113},{2,50},{3,115},{4,116},{5,53},{6,118},{7,55},{8,56}... | collective-permute-start | bytes 491528 | tf_op jit(solution)/shard_map/ppermute | solution.py:45
  55.1 3.6 %collective-permute-done.16 = f32[1,232,256]{2,1,0:T(8,128)S(1)} collective-permute-done((f32[1,232,256]{2,1,0:T(8,128)S(1)}, f32[1,232,256]{2,1,0:T(8,128)S(1)}, u32[]{:S(2)}, u32[]{:S(2)}) %collective-permute-start.16) | collective-permute-done | bytes 237600 | tf_op jit(solution)/shard_map/ppermute | solution.py:45
  59.3 2.0 %collective-permute-start.6 = (f32[1,192,256]{2,1,0:T(8,128)S(1)}, f32[1,192,256]{2,1,0:T(8,128)S(1)}, u32[]{:S(2)}, u32[]{:S(2)}) collective-permute-start(f32[1,192,256]{2,1,0:T(8,128)S(1)} %add.68), channel_id=1, source_target_pairs={{0,48},{1,113},{2,50},{3,115},{4,116},{5,53},{6,118},{7,55},{8,56}... | collective-permute-start | bytes 589832 | tf_op jit(solution)/shard_map/ppermute | solution.py:45
  61.4 3.0 %collective-permute-start.25 = (f32[1,160,256]{2,1,0:T(8,128)S(1)}, f32[1,160,256]{2,1,0:T(8,128)S(1)}, u32[]{:S(2)}, u32[]{:S(2)}) collective-permute-start(f32[1,160,256]{2,1,0:T(8,128)S(1)} %add.81), channel_id=1, source_target_pairs={{0,17},{1,18},{2,19},{3,16},{4,23},{5,20},{6,21},{7,22},{8,25},{9,... | collective-permute-start | bytes 491528 | tf_op jit(solution)/shard_map/ppermute | solution.py:45
  64.4 3.3 %collective-permute-done.25 = f32[1,160,256]{2,1,0:T(8,128)S(1)} collective-permute-done((f32[1,160,256]{2,1,0:T(8,128)S(1)}, f32[1,160,256]{2,1,0:T(8,128)S(1)}, u32[]{:S(2)}, u32[]{:S(2)}) %collective-permute-start.25) | collective-permute-done | bytes 163872 | tf_op jit(solution)/shard_map/ppermute | solution.py:45
  67.9 2.8 %collective-permute-start.7 = (f32[1,192,256]{2,1,0:T(8,128)S(1)}, f32[1,192,256]{2,1,0:T(8,128)S(1)}, u32[]{:S(2)}, u32[]{:S(2)}) collective-permute-start(f32[1,192,256]{2,1,0:T(8,128)S(1)} %add.69), channel_id=1, source_target_pairs={{0,17},{1,18},{2,19},{3,16},{4,23},{5,20},{6,21},{7,22},{8,25},{9,... | collective-permute-start | bytes 589832 | tf_op jit(solution)/shard_map/ppermute | solution.py:45
  70.7 2.5 %collective-permute-start.18 = (f32[2,232,256]{2,1,0:T(8,128)S(1)}, f32[2,232,256]{2,1,0:T(8,128)S(1)}, u32[]{:S(2)}, u32[]{:S(2)}) collective-permute-start(f32[2,232,256]{2,1,0:T(8,128)S(1)} %pad_maximum_fusion.3), channel_id=1, source_target_pairs={{0,48},{1,113},{2,50},{3,115},{4,116},{5,53},{6,118},{7,55},{8,56}... | collective-permute-start | bytes 1425416 | tf_op jit(solution)/shard_map/ppermute | solution.py:45
  78.4 3.1 %collective-permute-start.28 = (f32[2,160,256]{2,1,0:T(8,128)S(1)}, f32[2,160,256]{2,1,0:T(8,128)S(1)}, u32[]{:S(2)}, u32[]{:S(2)}) collective-permute-start(f32[2,160,256]{2,1,0:T(8,128)S(1)} %pad_maximum_fusion.5), channel_id=1, source_target_pairs={{0,20},{1,29},{2,22},{3,31},{4,24},{5,17},{6,26},{7,19},{8,28},{9,... | collective-permute-start | bytes 983048 | tf_op jit(solution)/shard_map/ppermute | solution.py:45
  83.1 4.5 %collective-permute-start.9 = (f32[4,192,256]{2,1,0:T(8,128)S(1)}, f32[4,192,256]{2,1,0:T(8,128)S(1)}, u32[]{:S(2)}, u32[]{:S(2)}) collective-permute-start(f32[4,192,256]{2,1,0:T(8,128)S(1)} %pad_maximum_fusion.1.own), channel_id=1, source_target_pairs={{0,16},{1,17},{2,18},{3,19},{4,20},{5,21},{6,22},{7,23},{8,24},{9,... | collective-permute-start | bytes 2359304 | tf_op jit(solution)/shard_map/ppermute | solution.py:45
  87.7 1.9 %collective-permute-start.29 = (f32[4,160,256]{2,1,0:T(8,128)S(1)}, f32[4,160,256]{2,1,0:T(8,128)S(1)}, u32[]{:S(2)}, u32[]{:S(2)}) collective-permute-start(f32[4,160,256]{2,1,0:T(8,128)S(1)} %pad_maximum_fusion.2.own), channel_id=1, source_target_pairs={{0,16},{1,17},{2,18},{3,19},{4,20},{5,21},{6,22},{7,23},{8,24},{9,... | collective-permute-start | bytes 1966088 | tf_op jit(solution)/shard_map/ppermute | solution.py:45
  94.6 2.1 %shard_map.130 = (f32[2304,256]{1,0:T(8,128)}, f32[2304,256]{1,0:T(8,128)}) custom-call(f32[4,232,256]{2,1,0:T(8,128)S(1)} %pad_maximum_fusion.own, f32[4,232,256]{2,1,0:T(8,128)S(1)} %collective-permute-done.19.other, f32[1,8,256]{2,1,0:T(8,128)S(1)} %slice.60.counts, f32[2304,256]{1,0:T(8,128)S(1)} %copy-done.2, f32[2304,256]{1,0:T(8,128)S(1)} %copy-done.3), custom_call_target="tpu_custom_call" | custom-call | flops 7000000 | bytes 7000000 | tf_op jit(solution)/shard_map/pallas_call | solution.py:273
  (94 shorter events, 27.9 us)
Async XLA Ops:
  9.1 7.4 %collective-permute-start.10 = (f32[4,232,256]{2,1,0:T(8,128)S(1)}, f32[4,232,256]{2,1,0:T(8,128)S(1)}, u32[]{:S(2)}, u32[]{:S(2)}) collective-permute-start(f32[4,232,256]{2,1,0:T(8,128)S(1)} %get-tuple-element.25), channel_id=1, source_target_pairs={{0,16},{1,17},{2,18},{3,19},{4,20},{5,21},{6,22},{7,23},{8,24},{9,... | collective-permute-start | bytes 2850824 | tf_op jit(solution)/shard_map/ppermute | solution.py:45
  13.0 6.3 %collective-permute-start = (f32[4,192,256]{2,1,0:T(8,128)S(1)}, f32[4,192,256]{2,1,0:T(8,128)S(1)}, u32[]{:S(2)}, u32[]{:S(2)}) collective-permute-start(f32[4,192,256]{2,1,0:T(8,128)S(1)} %get-tuple-element.23), channel_id=1, source_target_pairs={{0,16},{1,17},{2,18},{3,19},{4,20},{5,21},{6,22},{7,23},{8,24},{9,... | collective-permute-start | bytes 2359304 | tf_op jit(solution)/shard_map/ppermute | solution.py:45
  16.7 9.7 %collective-permute-start.11 = (f32[2,232,256]{2,1,0:T(8,128)S(1)}, f32[2,232,256]{2,1,0:T(8,128)S(1)}, u32[]{:S(2)}, u32[]{:S(2)}) collective-permute-start(f32[2,232,256]{2,1,0:T(8,128)S(1)} %slice.57), channel_id=1, source_target_pairs={{0,48},{1,113},{2,50},{3,115},{4,116},{5,53},{6,118},{7,55},{8,56}... | collective-permute-start | bytes 1425416 | tf_op jit(solution)/shard_map/ppermute | solution.py:45
  19.4 7.6 %collective-permute-start.1 = (f32[2,192,256]{2,1,0:T(8,128)S(1)}, f32[2,192,256]{2,1,0:T(8,128)S(1)}, u32[]{:S(2)}, u32[]{:S(2)}) collective-permute-start(f32[2,192,256]{2,1,0:T(8,128)S(1)} %slice.53), channel_id=1, source_target_pairs={{0,19},{1,16},{2,17},{3,18},{4,21},{5,22},{6,23},{7,20},{8,27},{9,... | collective-permute-start | bytes 1179656 | tf_op jit(solution)/shard_map/ppermute | solution.py:45
  21.3 18.4 %collective-permute-start.21 = (f32[2,160,256]{2,1,0:T(8,128)S(1)}, f32[2,160,256]{2,1,0:T(8,128)S(1)}, u32[]{:S(2)}, u32[]{:S(2)}) collective-permute-start(f32[2,160,256]{2,1,0:T(8,128)S(1)} %slice.62), channel_id=1, source_target_pairs={{0,20},{1,29},{2,22},{3,31},{4,24},{5,17},{6,26},{7,19},{8,28},{9,... | collective-permute-start | bytes 983048 | tf_op jit(solution)/shard_map/ppermute | solution.py:45
  26.4 5.9 %collective-permute-start.12 = (f32[1,232,256]{2,1,0:T(8,128)S(1)}, f32[1,232,256]{2,1,0:T(8,128)S(1)}, u32[]{:S(2)}, u32[]{:S(2)}) collective-permute-start(f32[1,232,256]{2,1,0:T(8,128)S(1)} %slice.59), channel_id=1, source_target_pairs={{0,112},{1,49},{2,114},{3,51},{4,52},{5,117},{6,54},{7,119},{8,120... | collective-permute-start | bytes 712712 | tf_op jit(solution)/shard_map/ppermute | solution.py:45
  27.1 7.6 %collective-permute-start.2 = (f32[1,192,256]{2,1,0:T(8,128)S(1)}, f32[1,192,256]{2,1,0:T(8,128)S(1)}, u32[]{:S(2)}, u32[]{:S(2)}) collective-permute-start(f32[1,192,256]{2,1,0:T(8,128)S(1)} %slice.55), channel_id=1, source_target_pairs={{0,17},{1,18},{2,19},{3,16},{4,23},{5,20},{6,21},{7,22},{8,25},{9,... | collective-permute-start | bytes 589832 | tf_op jit(solution)/shard_map/ppermute | solution.py:45
  32.4 7.1 %collective-permute-start.13 = (f32[1,232,256]{2,1,0:T(8,128)S(1)}, f32[1,232,256]{2,1,0:T(8,128)S(1)}, u32[]{:S(2)}, u32[]{:S(2)}) collective-permute-start(f32[1,232,256]{2,1,0:T(8,128)S(1)} %slice_add_fusion.3), channel_id=1, source_target_pairs={{0,17},{1,18},{2,19},{3,16},{4,23},{5,20},{6,21},{7,22},{8,25},{9,... | collective-permute-start | bytes 712712 | tf_op jit(solution)/shard_map/ppermute | solution.py:45
  34.7 6.9 %collective-permute-start.3 = (f32[1,192,256]{2,1,0:T(8,128)S(1)}, f32[1,192,256]{2,1,0:T(8,128)S(1)}, u32[]{:S(2)}, u32[]{:S(2)}) collective-permute-start(f32[1,192,256]{2,1,0:T(8,128)S(1)} %slice_add_fusion.4), channel_id=1, source_target_pairs={{0,28},{1,21},{2,30},{3,23},{4,16},{5,25},{6,18},{7,27},{8,20},{9,... | collective-permute-start | bytes 589832 | tf_op jit(solution)/shard_map/ppermute | solution.py:45
  39.7 9.2 %collective-permute-start.22 = (f32[1,160,256]{2,1,0:T(8,128)S(1)}, f32[1,160,256]{2,1,0:T(8,128)S(1)}, u32[]{:S(2)}, u32[]{:S(2)}) collective-permute-start(f32[1,160,256]{2,1,0:T(8,128)S(1)} %slice.64), channel_id=1, source_target_pairs={{0,28},{1,21},{2,30},{3,23},{4,16},{5,25},{6,18},{7,27},{8,20},{9,... | collective-permute-start | bytes 491528 | tf_op jit(solution)/shard_map/ppermute | solution.py:45
  41.6 11.2 %collective-permute-start.4 = (f32[1,192,256]{2,1,0:T(8,128)S(1)}, f32[1,192,256]{2,1,0:T(8,128)S(1)}, u32[]{:S(2)}, u32[]{:S(2)}) collective-permute-start(f32[1,192,256]{2,1,0:T(8,128)S(1)} %add.66), channel_id=1, source_target_pairs={{0,20},{1,29},{2,22},{3,31},{4,24},{5,17},{6,26},{7,19},{8,28},{9,... | collective-permute-start | bytes 589832 | tf_op jit(solution)/shard_map/ppermute | solution.py:45
  45.2 7.5 %collective-permute-start.15 = (f32[1,232,256]{2,1,0:T(8,128)S(1)}, f32[1,232,256]{2,1,0:T(8,128)S(1)}, u32[]{:S(2)}, u32[]{:S(2)}) collective-permute-start(f32[1,232,256]{2,1,0:T(8,128)S(1)} %add.74), channel_id=1, source_target_pairs={{0,20},{1,29},{2,22},{3,31},{4,24},{5,17},{6,26},{7,19},{8,28},{9,... | collective-permute-start | bytes 712712 | tf_op jit(solution)/shard_map/ppermute | solution.py:45
  49.0 6.0 %collective-permute-start.23 = (f32[1,160,256]{2,1,0:T(8,128)S(1)}, f32[1,160,256]{2,1,0:T(8,128)S(1)}, u32[]{:S(2)}, u32[]{:S(2)}) collective-permute-start(f32[1,160,256]{2,1,0:T(8,128)S(1)} %slice_add_fusion.5), channel_id=1, source_target_pairs={{0,48},{1,113},{2,50},{3,115},{4,116},{5,53},{6,118},{7,55},{8,56}... | collective-permute-start | bytes 491528 | tf_op jit(solution)/shard_map/ppermute | solution.py:45
  52.9 6.4 %collective-permute-start.5 = (f32[1,192,256]{2,1,0:T(8,128)S(1)}, f32[1,192,256]{2,1,0:T(8,128)S(1)}, u32[]{:S(2)}, u32[]{:S(2)}) collective-permute-start(f32[1,192,256]{2,1,0:T(8,128)S(1)} %add.67), channel_id=1, source_target_pairs={{0,112},{1,49},{2,114},{3,51},{4,52},{5,117},{6,54},{7,119},{8,120... | collective-permute-start | bytes 589832 | tf_op jit(solution)/shard_map/ppermute | solution.py:45
  55.0 6.3 %collective-permute-start.24 = (f32[1,160,256]{2,1,0:T(8,128)S(1)}, f32[1,160,256]{2,1,0:T(8,128)S(1)}, u32[]{:S(2)}, u32[]{:S(2)}) collective-permute-start(f32[1,160,256]{2,1,0:T(8,128)S(1)} %add.80), channel_id=1, source_target_pairs={{0,112},{1,49},{2,114},{3,51},{4,52},{5,117},{6,54},{7,119},{8,120... | collective-permute-start | bytes 491528 | tf_op jit(solution)/shard_map/ppermute | solution.py:45
  58.7 12.0 %collective-permute-start.17 = (f32[1,232,256]{2,1,0:T(8,128)S(1)}, f32[1,232,256]{2,1,0:T(8,128)S(1)}, u32[]{:S(2)}, u32[]{:S(2)}) collective-permute-start(f32[1,232,256]{2,1,0:T(8,128)S(1)} %add.76), channel_id=1, source_target_pairs={{0,112},{1,49},{2,114},{3,51},{4,52},{5,117},{6,54},{7,119},{8,120... | collective-permute-start | bytes 712712 | tf_op jit(solution)/shard_map/ppermute | solution.py:45
  59.3 8.5 %collective-permute-start.6 = (f32[1,192,256]{2,1,0:T(8,128)S(1)}, f32[1,192,256]{2,1,0:T(8,128)S(1)}, u32[]{:S(2)}, u32[]{:S(2)}) collective-permute-start(f32[1,192,256]{2,1,0:T(8,128)S(1)} %add.68), channel_id=1, source_target_pairs={{0,48},{1,113},{2,50},{3,115},{4,116},{5,53},{6,118},{7,55},{8,56}... | collective-permute-start | bytes 589832 | tf_op jit(solution)/shard_map/ppermute | solution.py:45
  61.4 6.3 %collective-permute-start.25 = (f32[1,160,256]{2,1,0:T(8,128)S(1)}, f32[1,160,256]{2,1,0:T(8,128)S(1)}, u32[]{:S(2)}, u32[]{:S(2)}) collective-permute-start(f32[1,160,256]{2,1,0:T(8,128)S(1)} %add.81), channel_id=1, source_target_pairs={{0,17},{1,18},{2,19},{3,16},{4,23},{5,20},{6,21},{7,22},{8,25},{9,... | collective-permute-start | bytes 491528 | tf_op jit(solution)/shard_map/ppermute | solution.py:45
  67.9 7.0 %collective-permute-start.7 = (f32[1,192,256]{2,1,0:T(8,128)S(1)}, f32[1,192,256]{2,1,0:T(8,128)S(1)}, u32[]{:S(2)}, u32[]{:S(2)}) collective-permute-start(f32[1,192,256]{2,1,0:T(8,128)S(1)} %add.69), channel_id=1, source_target_pairs={{0,17},{1,18},{2,19},{3,16},{4,23},{5,20},{6,21},{7,22},{8,25},{9,... | collective-permute-start | bytes 589832 | tf_op jit(solution)/shard_map/ppermute | solution.py:45
  70.7 10.7 %collective-permute-start.18 = (f32[2,232,256]{2,1,0:T(8,128)S(1)}, f32[2,232,256]{2,1,0:T(8,128)S(1)}, u32[]{:S(2)}, u32[]{:S(2)}) collective-permute-start(f32[2,232,256]{2,1,0:T(8,128)S(1)} %pad_maximum_fusion.3), channel_id=1, source_target_pairs={{0,48},{1,113},{2,50},{3,115},{4,116},{5,53},{6,118},{7,55},{8,56}... | collective-permute-start | bytes 1425416 | tf_op jit(solution)/shard_map/ppermute | solution.py:45
  74.9 8.2 %collective-permute-start.8 = (f32[2,192,256]{2,1,0:T(8,128)S(1)}, f32[2,192,256]{2,1,0:T(8,128)S(1)}, u32[]{:S(2)}, u32[]{:S(2)}) collective-permute-start(f32[2,192,256]{2,1,0:T(8,128)S(1)} %pad_maximum_fusion.4), channel_id=1, source_target_pairs={{0,19},{1,16},{2,17},{3,18},{4,21},{5,22},{6,23},{7,20},{8,27},{9,... | collective-permute-start | bytes 1179656 | tf_op jit(solution)/shard_map/ppermute | solution.py:45
  78.4 9.2 %collective-permute-start.28 = (f32[2,160,256]{2,1,0:T(8,128)S(1)}, f32[2,160,256]{2,1,0:T(8,128)S(1)}, u32[]{:S(2)}, u32[]{:S(2)}) collective-permute-start(f32[2,160,256]{2,1,0:T(8,128)S(1)} %pad_maximum_fusion.5), channel_id=1, source_target_pairs={{0,20},{1,29},{2,22},{3,31},{4,24},{5,17},{6,26},{7,19},{8,28},{9,... | collective-permute-start | bytes 983048 | tf_op jit(solution)/shard_map/ppermute | solution.py:45
  81.5 11.4 %collective-permute-start.19 = (f32[4,232,256]{2,1,0:T(8,128)S(1)}, f32[4,232,256]{2,1,0:T(8,128)S(1)}, u32[]{:S(2)}, u32[]{:S(2)}) collective-permute-start(f32[4,232,256]{2,1,0:T(8,128)S(1)} %pad_maximum_fusion.own), channel_id=1, source_target_pairs={{0,16},{1,17},{2,18},{3,19},{4,20},{5,21},{6,22},{7,23},{8,24},{9,... | collective-permute-start | bytes 2850824 | tf_op jit(solution)/shard_map/ppermute | solution.py:45
  83.1 6.4 %collective-permute-start.9 = (f32[4,192,256]{2,1,0:T(8,128)S(1)}, f32[4,192,256]{2,1,0:T(8,128)S(1)}, u32[]{:S(2)}, u32[]{:S(2)}) collective-permute-start(f32[4,192,256]{2,1,0:T(8,128)S(1)} %pad_maximum_fusion.1.own), channel_id=1, source_target_pairs={{0,16},{1,17},{2,18},{3,19},{4,20},{5,21},{6,22},{7,23},{8,24},{9,... | collective-permute-start | bytes 2359304 | tf_op jit(solution)/shard_map/ppermute | solution.py:45
  (14 other events, 74.7 us)
